TPU v7x, 32 devices: a whole 2x2x4 slice. The times are simulated.
32 devices in a mesh: groups: 2 (over y), batch: 4 (over z), blk: 4 (over x, core).
Axes of the slice: x: 2, y: 2, z: 4, core: 2. Of those that a mesh axis runs over, the one named last changes fastest.
Arguments:
- queries: bfloat16 [8, 592, 1024], P(('groups', 'batch'), 'blk'), parts along dimension 0, may hold values from -12 to 12
- key_states: bfloat16 [8, 592, 1024], P(('groups', 'batch'), 'blk'), parts along dimension 0, may hold values from -6 to 6
- value_states: bfloat16 [8, 592, 1024], P(('groups', 'batch'), 'blk'), parts along dimension 0, may hold values from -6 to 6
- residual: bfloat16 [8, 592, 768], P(('groups', 'batch'), 'blk'), parts along dimension 0, may hold values from -3 to 3
- proj_weight: bfloat16 [1024, 768], P(None, 'batch'), may hold values from -0.1875 to 0.1875
- conv_weight: bfloat16 [3, 3, 768, 384], P(None, None, 'batch'), may hold values from -0.078125 to 0.078125
Outputs:
- conv_out: bfloat16 [8, 592, 384], P(('groups', 'batch'), 'blk'), parts along dimension 0
There are 2 independent parts, one for each index of `groups`. A program takes and returns all parts, laid end to end along the dimension named above; an argument that names none is the same for every part. Nothing has to cross between parts.
All inputs are finite; a program needn't handle non-finite values.
Results may differ from a plain program's by a relative error of at most 0.0085.
Values may be sent and summed in bfloat16 or wider, within the bound.
A program may use at most 64 MiB of HBM per device.

v0:
```python
import jax
import jax.numpy as jnp
from jax import lax
from jax.sharding import PartitionSpec as P

HEADS = 16
HD = 64
COLS = 74
ROWS = 2


def extended(cells, sides, width):
    for axis, dim in sides:
        count = lax.axis_size(axis)
        ends = count - 1
        head = lax.slice_in_dim(cells, 0, width, axis=dim)
        tail = lax.slice_in_dim(cells, cells.shape[dim] - width, cells.shape[dim], axis=dim)
        cells = jnp.concatenate(
            [
                lax.ppermute(tail, axis, [(i, (i + 1) % count) for i in range(ends)]),
                cells,
                lax.ppermute(head, axis, [((i + 1) % count, i) for i in range(ends)]),
            ],
            axis=dim,
        )
    return cells


def empty_state(head_count, query_rows):
    return (
        jnp.full((head_count, query_rows), -1e30, jnp.float32),
        jnp.zeros((head_count, query_rows), jnp.float32),
        jnp.zeros((head_count, query_rows, HD), jnp.float32),
    )


def absorb(carry_state, query_block, key_block, value_block):
    row_max, weight_sum, running = carry_state
    scores = jnp.einsum(
        "qhd,khd->hqk", query_block, key_block, preferred_element_type=jnp.float32
    ) * HD ** (-0.5)
    new_max = jnp.maximum(row_max, jnp.max(scores, axis=2))
    factor = jnp.exp(row_max - new_max)
    weights = jnp.exp(scores - new_max[:, :, None])
    weight_sum = weight_sum * factor + jnp.sum(weights, axis=2)
    running = running * factor[:, :, None] + jnp.einsum(
        "hqk,khd->hqd",
        weights.astype(jnp.bfloat16),
        value_block,
        preferred_element_type=jnp.float32,
    )
    return (new_max, weight_sum, running)


def finish(carry_state):
    row_max, weight_sum, running = carry_state
    mixed = running / weight_sum[:, :, None]
    head_count, query_rows = weight_sum.shape
    return mixed.transpose(1, 0, 2).reshape(query_rows, head_count * HD).astype(jnp.bfloat16)


def body(queries, key_states, value_states, residual, proj_weight, conv_weight):
    query_rows = queries[0]
    key_rows = key_states[0]
    value_rows = value_states[0]
    tok_rows = query_rows.shape[0]
    cycle_count = lax.axis_size("blk")
    local_heads = HEADS // cycle_count
    query_all, key_all, value_all = (
        lax.all_to_all(query_rows, "blk", split_axis=1, concat_axis=0, tiled=True),
        lax.all_to_all(key_rows, "blk", split_axis=1, concat_axis=0, tiled=True),
        lax.all_to_all(value_rows, "blk", split_axis=1, concat_axis=0, tiled=True),
    )
    seq_rows = tok_rows * cycle_count
    group = 1
    while cycle_count % (group * 2) == 0 and tok_rows * group * 2 <= 1024:
        group = group * 2
    block_rows = tok_rows * group
    block_count = seq_rows // block_rows
    query_blocks = query_all.reshape(block_count, block_rows, local_heads, HD)
    key_blocks = key_all.reshape(block_count, block_rows, local_heads, HD)
    value_blocks = value_all.reshape(block_count, block_rows, local_heads, HD)

    def one_block(query_block):

        def absorb_one(index, inner_state):
            return absorb(inner_state, query_block, key_blocks[index], value_blocks[index])

        return finish(
            lax.fori_loop(0, block_count, absorb_one, empty_state(local_heads, block_rows))
        )

    mixed_rows = lax.map(one_block, query_blocks).reshape(seq_rows, local_heads * HD)
    attention = lax.all_to_all(mixed_rows, "blk", split_axis=0, concat_axis=1, tiled=True)
    projected = jnp.dot(
        attention,
        lax.all_gather(proj_weight, "batch", axis=1, tiled=True),
        preferred_element_type=jnp.float32,
    )
    hidden = (residual[0].astype(jnp.float32) + projected).astype(jnp.bfloat16)
    feature_grid = hidden.reshape(ROWS, COLS, hidden.shape[1])
    rimmed = extended(feature_grid, (("blk", 0),), 1)
    padded = jnp.pad(rimmed, ((0, 0), (1, 1), (0, 0)))
    shard_piece = lax.all_gather(conv_weight, "batch", axis=2, tiled=True)
    piece_rows = shard_piece.shape[2]
    windows = []
    for row_off in range(3):
        for col_off in range(3):
            windows.append(
                padded[row_off : row_off + ROWS, col_off : col_off + COLS].reshape(
                    tok_rows, piece_rows
                )
            )
    stacked = jnp.concatenate(windows, axis=1)
    flat_weight = shard_piece.reshape(9 * piece_rows, shard_piece.shape[3])
    conv_sum = jnp.dot(stacked, flat_weight, preferred_element_type=jnp.float32)
    return conv_sum.astype(jnp.bfloat16)[None]


def solution(mesh):
    return jax.shard_map(
        body,
        mesh=mesh,
        in_specs=(
            P(("groups", "batch"), "blk", None),
            P(("groups", "batch"), "blk", None),
            P(("groups", "batch"), "blk", None),
            P(("groups", "batch"), "blk", None),
            P(None, "batch"),
            P(None, None, "batch", None),
        ),
        out_specs=P(("groups", "batch"), "blk", None),
        check_vma=False,
    )
```

profile of v0, /device:TPU:0, one launch (start us, length us, event | category | flops | bytes accessed | tf_op | source)
XLA Modules:
  0.0 159.6 jit_solution(15283503268794246920)
XLA Ops:
  8.0 1.2 all_to_all.48
  9.9 4.2 %all-to-all-start = ((bf16[148,4,256]{2,0,1:T(8,128)(2,1)}), bf16[148,4,256]{2,0,1:T(8,128)(2,1)S(1)}, u32[]{:S(2)}, u32[]{:S(2)}) async-start(bf16[148,4,256]{2,0,1:T(8,128)(2,1)} %copy.22), calls=%async_computation | async-start | bytes 622592 | tf_op jit(solution)/shard_map/all_to_all | solution.py:70
  14.3 0.8 copy.24
  15.1 5.6 %all-to-all-done = bf16[148,4,256]{2,0,1:T(8,128)(2,1)S(1)} async-done(((bf16[148,4,256]{2,0,1:T(8,128)(2,1)}), bf16[148,4,256]{2,0,1:T(8,128)(2,1)S(1)}, u32[]{:S(2)}, u32[]{:S(2)}) %all-to-all-start) | async-done | bytes 303136 | tf_op jit(solution)/shard_map/all_to_all | solution.py:70
  20.7 3.5 %all-to-all-start.1 = ((bf16[148,4,256]{2,0,1:T(8,128)(2,1)}), bf16[148,4,256]{2,0,1:T(8,128)(2,1)S(1)}, u32[]{:S(2)}, u32[]{:S(2)}) async-start(bf16[148,4,256]{2,0,1:T(8,128)(2,1)} %copy.24), calls=%async_computation.1 | async-start | bytes 622592 | tf_op jit(solution)/shard_map/all_to_all | solution.py:71
  25.0 5.6 %all-to-all-done.1 = bf16[148,4,256]{2,0,1:T(8,128)(2,1)S(1)} async-done(((bf16[148,4,256]{2,0,1:T(8,128)(2,1)}), bf16[148,4,256]{2,0,1:T(8,128)(2,1)S(1)}, u32[]{:S(2)}, u32[]{:S(2)}) %all-to-all-start.1) | async-done | bytes 303136 | tf_op jit(solution)/shard_map/all_to_all | solution.py:71
  30.6 3.5 %all-to-all-start.2 = ((bf16[148,4,256]{2,0,1:T(8,128)(2,1)}), bf16[148,4,256]{2,0,1:T(8,128)(2,1)S(1)}, u32[]{:S(2)}, u32[]{:S(2)}) async-start(bf16[148,4,256]{2,0,1:T(8,128)(2,1)} %copy.26), calls=%async_computation.2 | async-start | bytes 622592 | tf_op jit(solution)/shard_map/all_to_all | solution.py:72
  34.7 5.9 %all-to-all-done.2 = bf16[148,4,256]{2,0,1:T(8,128)(2,1)S(1)} async-done(((bf16[148,4,256]{2,0,1:T(8,128)(2,1)}), bf16[148,4,256]{2,0,1:T(8,128)(2,1)S(1)}, u32[]{:S(2)}, u32[]{:S(2)}) %all-to-all-start.2) | async-done | bytes 303136 | tf_op jit(solution)/shard_map/all_to_all | solution.py:72
  40.9 1.1 multiply_reduce_fusion
  42.0 1.0 fusion
  43.1 1.3 fusion.17
  45.1 8.9 %all_to_all.64 = bf16[4,148,256]{2,1,0:T(8,128)(2,1)S(1)} all-to-all(bf16[4,148,256]{2,1,0:T(8,128)(2,1)S(1)} %copy.29), channel_id=1, replica_groups=mesh['groups'=2,'batch'=4,'blk'=4] {'blk'}, dimensions={0} | all-to-all | bytes 606208 | tf_op jit(solution)/shard_map/all_to_all | solution.py:94
  54.3 2.2 %fusion.12 = bf16[148,768]{1,0:T(8,128)(2,1)S(1)} fusion(bf16[148,1024]{1,0:T(8,128)(2,1)S(1)} %bitcast.41, bf16[1024,768]{0,1:T(8,128)(2,1)} %all-gather.3.cloned.1.call-done, bf16[1,148,768]{2,1,0:T(8,128)(2,1)S(1)} %copy-done.2), kind=kOutput, calls=%fused_computation.12 | convolution fusion | flops 233124864 | bytes 2330624 | tf_op jit(solution)/shard_map/dot_general | solution.py:95
  56.5 1.7 %collective-permute-start = (bf16[1,74,768]{2,1,0:T(8,128)(2,1)S(1)}, bf16[1,74,768]{2,1,0:T(8,128)(2,1)S(1)}, u32[]{:S(2)}, u32[]{:S(2)}) collective-permute-start(bf16[1,74,768]{2,1,0:T(8,128)(2,1)S(1)} %get-tuple-element.60), channel_id=1, source_target_pairs={{0,1},{1,2},{2,3},{4,5},{5,6},{6,7},{8,9},{9,10},{10,11},{12,13},{... | collective-permute-start | bytes 341000 | tf_op jit(solution)/shard_map/ppermute | solution.py:20
  58.2 1.3 collective-permute-start.1
  59.6 2.0 %collective-permute-done.1 = bf16[1,74,768]{2,1,0:T(8,128)(2,1)S(1)} collective-permute-done((bf16[1,74,768]{2,1,0:T(8,128)(2,1)S(1)}, bf16[1,74,768]{2,1,0:T(8,128)(2,1)S(1)}, u32[]{:S(2)}, u32[]{:S(2)}) %collective-permute-start.1) | collective-permute-done | bytes 113696 | tf_op jit(solution)/shard_map/ppermute | solution.py:22
  62.0 0.8 reshape.82
  62.8 0.8 reshape.83
  63.5 0.8 reshape.84
  64.5 1.0 constant_dynamic-update-slice_fusion.7
  65.5 1.0 constant_dynamic-update-slice_fusion.6
  66.5 1.0 constant_dynamic-update-slice_fusion.5
  67.5 80.7 %all-gather.5.cloned.1.call-done = bf16[3,3,768,384]{3,2,1,0:T(8,128)(2,1)} async-done(((bf16[3,3,192,384]{3,2,1,0:T(8,128)(2,1)}), bf16[3,3,768,384]{3,2,1,0:T(8,128)(2,1)}) %all-gather.5.cloned.1.call-update) | async-done | bytes 5308432 | tf_op jit(solution)/shard_map/all_gather | solution.py:104
  148.3 4.5 %fusion.13 = bf16[1,148,384]{2,1,0:T(8,128)(2,1)} fusion(bf16[148,6912]{1,0:T(8,128)(2,1)S(1)} %constant_dynamic-update-slice_fusion, bf16[6912,384]{1,0:T(8,128)(2,1)} %bitcast.37), kind=kOutput, calls=%fused_computation.14 | convolution fusion | flops 785702400 | bytes 7468032 | tf_op jit(solution)/shard_map/dot_general | solution.py:116
  (42 shorter events, 5.8 us)
Async XLA Ops:
  6.5 7.6 %copy-start = (bf16[1,148,1024]{2,1,0:T(8,128)(2,1)S(1)}, bf16[1,148,1024]{2,1,0:T(8,128)(2,1)}, u32[]{:S(2)}) copy-start(bf16[1,148,1024]{2,1,0:T(8,128)(2,1)} %param.7) | copy-start | bytes 909316
  6.5 47.8 %all-gather.3.cloned.1.call-start = ((), (), s32[]{:S(2)}) async-start(), calls=%async_computation.4 | async-start | bytes 1966080 | tf_op jit(solution)/shard_map/all_gather | solution.py:97
  7.3 141.0 %all-gather.5.cloned.1.call-start = ((), (), s32[]{:S(2)}) async-start(), calls=%async_computation.5 | async-start | bytes 6635520 | tf_op jit(solution)/shard_map/all_gather | solution.py:104
  8.0 16.1 %copy-start.1 = (bf16[1,148,1024]{2,1,0:T(8,128)(2,1)S(1)}, bf16[1,148,1024]{2,1,0:T(8,128)(2,1)}, u32[]{:S(2)}) copy-start(bf16[1,148,1024]{2,1,0:T(8,128)(2,1)} %param.8) | copy-start | bytes 909316
  9.9 10.8 %all-to-all-start = ((bf16[148,4,256]{2,0,1:T(8,128)(2,1)}), bf16[148,4,256]{2,0,1:T(8,128)(2,1)S(1)}, u32[]{:S(2)}, u32[]{:S(2)}) async-start(bf16[148,4,256]{2,0,1:T(8,128)(2,1)} %copy.22), calls=%async_computation | async-start | bytes 622592 | tf_op jit(solution)/shard_map/all_to_all | solution.py:70
  20.7 10.0 %all-to-all-start.1 = ((bf16[148,4,256]{2,0,1:T(8,128)(2,1)}), bf16[148,4,256]{2,0,1:T(8,128)(2,1)S(1)}, u32[]{:S(2)}, u32[]{:S(2)}) async-start(bf16[148,4,256]{2,0,1:T(8,128)(2,1)} %copy.24), calls=%async_computation.1 | async-start | bytes 622592 | tf_op jit(solution)/shard_map/all_to_all | solution.py:71
  30.6 10.0 %all-to-all-start.2 = ((bf16[148,4,256]{2,0,1:T(8,128)(2,1)}), bf16[148,4,256]{2,0,1:T(8,128)(2,1)S(1)}, u32[]{:S(2)}, u32[]{:S(2)}) async-start(bf16[148,4,256]{2,0,1:T(8,128)(2,1)} %copy.26), calls=%async_computation.2 | async-start | bytes 622592 | tf_op jit(solution)/shard_map/all_to_all | solution.py:72
  44.4 9.9 %copy-start.2 = (bf16[1,148,768]{2,1,0:T(8,128)(2,1)S(1)}, bf16[1,148,768]{2,1,0:T(8,128)(2,1)}, u32[]{:S(2)}) copy-start(bf16[1,148,768]{2,1,0:T(8,128)(2,1)} %param.9) | copy-start | bytes 681988
  56.5 3.0 %collective-permute-start = (bf16[1,74,768]{2,1,0:T(8,128)(2,1)S(1)}, bf16[1,74,768]{2,1,0:T(8,128)(2,1)S(1)}, u32[]{:S(2)}, u32[]{:S(2)}) collective-permute-start(bf16[1,74,768]{2,1,0:T(8,128)(2,1)S(1)} %get-tuple-element.60), channel_id=1, source_target_pairs={{0,1},{1,2},{2,3},{4,5},{5,6},{6,7},{8,9},{9,10},{10,11},{12,13},{... | collective-permute-start | bytes 341000 | tf_op jit(solution)/shard_map/ppermute | solution.py:20
  58.2 3.4 %collective-permute-start.1 = (bf16[1,74,768]{2,1,0:T(8,128)(2,1)S(1)}, bf16[1,74,768]{2,1,0:T(8,128)(2,1)S(1)}, u32[]{:S(2)}, u32[]{:S(2)}) collective-permute-start(bf16[1,74,768]{2,1,0:T(8,128)(2,1)S(1)} %get-tuple-element.61), channel_id=1, source_target_pairs={{1,0},{2,1},{3,2},{5,4},{6,5},{7,6},{9,8},{10,9},{11,10},{13,12},{... | collective-permute-start | bytes 341000 | tf_op jit(solution)/shard_map/ppermute | solution.py:22
Sparse Core Ops, SparseCore 0:
  8.9 39.7 all-gather.2
  50.2 97.9 all-gather.4
where the time goes:
time: 160 us
  waiting for transfers between devices  101 us (63%)
  starting transfers between devices  14.1 us (9%)
  between operations  13.7 us (9%)
  local copies, waits for them, and re-layouts  11.2 us (7%)
  matrix products  9.04 us (6%)
  blocking collectives  8.9 us (6%)
    all_gather x1, waiting for transfers between devices, body(): shard_piece = lax.all_gather(conv_weight, 'batch', axis=2, tiled=True)  80.7 us
    all_to_all x1, blocking collectives, body(): lax.all_to_all(mixed_rows, 'blk', split_axis=0, concat_axis=1, tiled=True)  8.9 us
    all_to_all x1, waiting for transfers between devices, body(): lax.all_to_all(value_rows, 'blk', split_axis=1, concat_axis=0, tiled=True)  5.92 us
    all_to_all x1, waiting for transfers between devices, body(): lax.all_to_all(query_rows, 'blk', split_axis=1, concat_axis=0, tiled=True)  5.62 us
    all_to_all x1, waiting for transfers between devices, body(): lax.all_to_all(key_rows, 'blk', split_axis=1, concat_axis=0, tiled=True)  5.6 us
    dot_general x1, matrix products, body(): conv_sum = jnp.dot(stacked, flat_weight, preferred_element_type=jnp.float32)  4.48 us
    all_to_all x1, starting transfers between devices, body(): lax.all_to_all(query_rows, 'blk', split_axis=1, concat_axis=0, tiled=True)  4.24 us
    all_to_all x1, starting transfers between devices, body(): lax.all_to_all(value_rows, 'blk', split_axis=1, concat_axis=0, tiled=True)  3.45 us
  transfers between devices with their start and end apart: 7, of which 5 were waited for; matrix products, arithmetic and copies ran while one was open for 10% of the time, Pallas kernels for 0%

commit v1 on v0

v1 whole, which is shorter than its diff:
```python
import functools

import jax
import jax.numpy as jnp
from jax import lax
from jax.experimental import pallas as pl
from jax.experimental.pallas import tpu as pltpu
from jax.sharding import PartitionSpec as P

HEADS = 16
HD = 64
COLS = 74
BASE = 8
MESH = pl.DeviceIdType.MESH


def kernel(G, Z, B, CI, NC, q_hbm, k_hbm, v_hbm, r_hbm, p_hbm, c_hbm, o_ref,
           q, res, kb, vb, wp, wc, att, hext, h_top, h_bot, r_top, r_bot, acc,
           lsem, ksend, krecv, kcs, kcr, zup, zdn, zrecv, ysend, yrecv, csend, crecv, hsend, hrecv):
    T = q.shape[0]
    X = B // 2
    g = lax.axis_index("groups")
    z = lax.axis_index("batch")
    b = lax.axis_index("blk")
    c = lax.rem(b, 2)
    x = b // 2
    mate = x * 2 + 1 - c
    NI = 1 + NC
    PP = wp.shape[1] // (2 * G)
    PC = wc.shape[1] // (2 * G)
    CC = PC // NC

    locals_ = [
        pltpu.make_async_copy(k_hbm, kb.at[b], lsem.at[0]),
        pltpu.make_async_copy(v_hbm, vb.at[b], lsem.at[1]),
        pltpu.make_async_copy(p_hbm, wp.at[z], lsem.at[2]),
        pltpu.make_async_copy(c_hbm, wc.at[z], lsem.at[3]),
        pltpu.make_async_copy(q_hbm, q, lsem.at[4]),
        pltpu.make_async_copy(r_hbm, res, lsem.at[5]),
    ]
    for copy in locals_:
        copy.start()

    barrier = pltpu.get_barrier_semaphore()

    def hello(where):
        pl.semaphore_signal(barrier, inc=1, device_id=where, device_id_type=MESH)

    for i in range(1, G):
        hello({"groups": lax.rem(g + i, G)})
    for i in range(1, X):
        hello({"blk": lax.rem(x + i, X) * 2 + c})
    hello({"blk": mate})
    pl.when(z > 0)(lambda: hello({"batch": z - 1}))
    pl.when(z < Z - 1)(lambda: hello({"batch": z + 1}))
    pl.when(b > 0)(lambda: hello({"blk": b - 1}))
    pl.when(b < B - 1)(lambda: hello({"blk": b + 1}))
    inner = (
        jnp.where(z > 0, 1, 0) + jnp.where(z < Z - 1, 1, 0)
        + jnp.where(b > 0, 1, 0) + jnp.where(b < B - 1, 1, 0)
    )
    pl.semaphore_wait(barrier, G - 1 + X - 1 + 1 + inner)

    def remote(ref, send, recv, where):
        return pltpu.make_async_remote_copy(
            src_ref=ref, dst_ref=ref, send_sem=send, recv_sem=recv,
            device_id=where, device_id_type=MESH,
        )

    kv = (kb, vb)

    def kv_out(w, i):
        return remote(kv[w].at[b], ksend.at[w, i], krecv.at[w, b // 2],
                      {"blk": lax.rem(x + i, X) * 2 + c})

    def kv_in(w, i):
        src = lax.rem(x + X - i, X)
        return remote(kv[w].at[src * 2 + c], ksend.at[w, i], krecv.at[w, src], {"blk": src * 2 + c})

    def kv_mate(w, i):
        src = lax.rem(x + X - i, X)
        return remote(kv[w].at[src * 2 + c], kcs.at[w, i], kcr.at[w, i], {"blk": mate})

    def kv_mate_in(w, i):
        src = lax.rem(x + X - i, X)
        return remote(kv[w].at[src * 2 + 1 - c], kcs.at[w, i], kcr.at[w, i], {"blk": mate})

    def item(j, s, p):
        if j == 0:
            return wp.at[s, pl.ds(pl.multiple_of(p * PP, 16), PP)]
        return wc.at[s, pl.ds(pl.multiple_of(p * PC + (j - 1) * CC, 16), CC)]

    mine = g * 2 + c

    def up(j, s):
        return remote(item(j, s, mine), zup.at[s, j], zrecv.at[s, j], {"batch": z + 1})

    def down(j, s):
        return remote(item(j, s, mine), zdn.at[s, j], zrecv.at[s, j], {"batch": z - 1})

    def side(j, s, i):
        return remote(item(j, s, mine), ysend.at[i, s, j], yrecv.at[i, s, j],
                      {"groups": lax.rem(g + i, G)})

    def side_in(j, s, i):
        other = lax.rem(g + G - i, G)
        return remote(item(j, s, other * 2 + c), ysend.at[i, s, j], yrecv.at[i, s, j],
                      {"groups": other})

    def cross(j, s, i):
        other = lax.rem(g + G - i, G)
        return remote(item(j, s, other * 2 + c), csend.at[i, s, j], crecv.at[i, s, j], {"blk": mate})

    def cross_in(j, s, i):
        other = lax.rem(g + G - i, G)
        return remote(item(j, s, other * 2 + 1 - c), csend.at[i, s, j], crecv.at[i, s, j], {"blk": mate})

    for w in range(2):
        locals_[w].wait()
        for i in range(1, X):
            kv_out(w, i).start()
        kv_mate(w, 0).start()
    locals_[2].wait()
    locals_[3].wait()
    for j in range(NI):
        pl.when(z < Z - 1)(lambda j=j: up(j, z).start())
        pl.when(z > 0)(lambda j=j: down(j, z).start())

    def arrived(j, d):
        @pl.when(z >= d)
        def _():
            s = z - d
            up(j, s).wait_recv()
            pl.when(z < Z - 1)(lambda: up(j, s).start())
            for i in range(1, G):
                side(j, s, i).start()
            cross(j, s, 0).start()

        @pl.when(z + d < Z)
        def _():
            s = z + d
            down(j, s).wait_recv()
            pl.when(z > 0)(lambda: down(j, s).start())
            for i in range(1, G):
                side(j, s, i).start()
            cross(j, s, 0).start()

    def relayed(j, d):
        for ok, s in ((z >= d, z - d), (z + d < Z, z + d)):
            @pl.when(ok)
            def _(s=s):
                for i in range(1, G):
                    side_in(j, s, i).wait_recv()
                    cross(j, s, i).start()

    def kv_pass(w):
        for i in range(1, X):
            kv_in(w, i).wait_recv()
            kv_mate(w, i).start()

    for d in range(1, Z):
        arrived(0, d)
    kv_pass(0)
    for j in range(1, NI):
        arrived(j, 1)
    kv_pass(1)
    for d in range(1, Z):
        relayed(0, d)
    for w in range(2):
        for i in range(X):
            kv_mate_in(w, i).wait_recv()
    locals_[4].wait()
    locals_[5].wait()

    first = lax.broadcasted_iota(jnp.int32, (1, 2 * HD), 1) < HD

    def pair(n, carry):
        cols = pl.ds(pl.multiple_of(n * 2 * HD, 2 * HD), 2 * HD)
        q2 = q[:, cols]
        outs = []
        for half in range(2):
            keep = first if half == 0 else jnp.logical_not(first)
            qh = jnp.where(keep, q2, jnp.zeros_like(q2))
            scores = [
                lax.dot_general(qh, kb[t, :, cols], (((1,), (1,)), ((), ())),
                                preferred_element_type=jnp.float32) * HD ** (-0.5)
                for t in range(B)
            ]
            top = functools.reduce(jnp.maximum, [jnp.max(s, axis=1, keepdims=True) for s in scores])
            total = jnp.zeros_like(top)
            mixed = jnp.zeros((T, 2 * HD), jnp.float32)
            for t in range(B):
                weights = jnp.exp(scores[t] - top)
                total = total + jnp.sum(weights, axis=1, keepdims=True)
                mixed = mixed + jnp.dot(weights.astype(jnp.bfloat16), vb[t, :, cols],
                                        preferred_element_type=jnp.float32)
            outs.append(mixed / total)
        att[:, cols] = jnp.where(first, outs[0], outs[1]).astype(jnp.bfloat16)
        return carry

    half_pairs = HEADS // 4
    lax.fori_loop(0, half_pairs, pair, 0)
    if Z > 2:
        arrived(1, 2)
    lax.fori_loop(half_pairs, HEADS // 2, pair, 0)
    if Z > 2:
        for j in range(2, NI):
            arrived(j, 2)
    for j in range(1, NI):
        relayed(j, 1)

    for d in range(1, Z):
        for ok, s in ((z >= d, z - d), (z + d < Z, z + d)):
            @pl.when(ok)
            def _(s=s):
                for i in range(G):
                    cross_in(0, s, i).wait_recv()
    own = BASE + COLS
    for s in range(Z):
        hidden = jnp.dot(att[...], wp[s], preferred_element_type=jnp.float32)
        hidden = hidden + res[:, s * CI:(s + 1) * CI].astype(jnp.float32)
        hidden = hidden.astype(jnp.bfloat16)
        wide = hidden.astype(jnp.float32)
        hext[s, own:own + T, :] = wide
        h_top[s] = hidden[:COLS]
        h_bot[s] = wide[T - COLS:].astype(jnp.bfloat16)

    def halo(src, dst, n, where):
        return pltpu.make_async_remote_copy(
            src_ref=src, dst_ref=dst, send_sem=hsend.at[n], recv_sem=hrecv.at[n],
            device_id={"blk": where}, device_id_type=MESH,
        )

    to_prev = lambda where: halo(h_top, r_bot, 0, where)
    to_next = lambda where: halo(h_bot, r_top, 1, where)
    pl.when(b > 0)(lambda: to_prev(b - 1).start())
    pl.when(b < B - 1)(lambda: to_next(b + 1).start())

    for d in range(3, Z):
        for j in range(1, NI):
            arrived(j, d)
            relayed(j, d - 1)
    if Z > 2:
        for j in range(1, NI):
            relayed(j, Z - 1)

    @pl.when(b > 0)
    def _():
        to_next(b - 1).wait_recv()
        for s in range(Z):
            hext[s, BASE:own, :] = r_top[s].astype(jnp.float32)

    @pl.when(b == 0)
    def _():
        for s in range(Z):
            hext[s, BASE:own, :] = jnp.zeros((COLS, CI), jnp.float32)

    @pl.when(b < B - 1)
    def _():
        to_prev(b + 1).wait_recv()
        for s in range(Z):
            hext[s, own + T:own + T + COLS, :] = r_bot[s].astype(jnp.float32)

    @pl.when(b == B - 1)
    def _():
        for s in range(Z):
            hext[s, own + T:own + T + COLS, :] = jnp.zeros((COLS, CI), jnp.float32)

    column = lax.rem(lax.broadcasted_iota(jnp.int32, (T, CI), 0), COLS)
    inside = (column != 0, None, column != COLS - 1)
    acc[...] = jnp.zeros_like(acc)

    def conv(n, carry):
        s = jnp.where(z * 2 < Z, lax.rem(z + n, Z), lax.rem(z - n + Z, Z))

        @pl.when(n > 0)
        def _():
            for j in range(1, NI):
                for i in range(G):
                    cross_in(j, s, i).wait_recv()

        total = acc[...]
        for row in range(3):
            for col in range(3):
                start = BASE + row * COLS + col - 1
                window = hext[s, start:start + T, :]
                if inside[col] is not None:
                    window = jnp.where(inside[col], window, 0.0)
                tap = row * 3 + col
                total = total + jnp.dot(window.astype(jnp.bfloat16), wc[s, tap * CI:(tap + 1) * CI, :],
                                        preferred_element_type=jnp.float32)
        acc[...] = total
        return carry

    lax.fori_loop(0, Z, conv, 0)
    o_ref[...] = acc[...].astype(jnp.bfloat16)

    for w in range(2):
        for i in range(1, X):
            kv_out(w, i).wait_send()
        for i in range(X):
            kv_mate(w, i).wait_send()
    pl.when(b > 0)(lambda: to_prev(b - 1).wait_send())
    pl.when(b < B - 1)(lambda: to_next(b + 1).wait_send())
    for j in range(NI):
        pl.when(z < Z - 1)(lambda j=j: up(j, z).wait_send())
        pl.when(z > 0)(lambda j=j: down(j, z).wait_send())
        for d in range(1, Z):
            @pl.when(z >= d)
            def _(j=j, d=d):
                pl.when(z < Z - 1)(lambda: up(j, z - d).wait_send())
                for i in range(1, G):
                    side(j, z - d, i).wait_send()
                for i in range(G):
                    cross(j, z - d, i).wait_send()

            @pl.when(z + d < Z)
            def _(j=j, d=d):
                pl.when(z > 0)(lambda: down(j, z + d).wait_send())
                for i in range(1, G):
                    side(j, z + d, i).wait_send()
                for i in range(G):
                    cross(j, z + d, i).wait_send()


def solution(mesh):
    G, Z, B = (mesh.shape[name] for name in ("groups", "batch", "blk"))

    def body(queries, key_states, value_states, residual, proj_weight, conv_weight):
        T = queries.shape[1]
        depth, CI = proj_weight.shape
        wide = residual.shape[2]
        taps = conv_weight.shape[0] * conv_weight.shape[1]
        out = conv_weight.shape[3]
        flat = conv_weight.reshape(taps * CI, out)
        unit = 2 * G * 16
        rows = -(-flat.shape[0] // unit) * unit
        if rows != flat.shape[0]:
            flat = jnp.pad(flat, ((0, rows - flat.shape[0]), (0, 0)))
        NC = 3 if (rows // unit) % 3 == 0 else 1
        NI = 1 + NC
        X = B // 2
        dma = pltpu.SemaphoreType.DMA
        bf16, f32 = jnp.bfloat16, jnp.float32
        result = pl.pallas_call(
            functools.partial(kernel, G, Z, B, CI, NC),
            out_shape=jax.ShapeDtypeStruct((T, out), bf16),
            in_specs=[pl.BlockSpec(memory_space=pl.ANY)] * 6,
            out_specs=pl.BlockSpec(memory_space=pltpu.VMEM),
            scratch_shapes=[
                pltpu.VMEM((T, depth), bf16),
                pltpu.VMEM((T, wide), bf16),
                pltpu.VMEM((B, T, depth), bf16),
                pltpu.VMEM((B, T, depth), bf16),
                pltpu.VMEM((Z, depth, CI), bf16),
                pltpu.VMEM((Z, rows, out), bf16),
                pltpu.VMEM((T, depth), bf16),
                pltpu.VMEM((Z, BASE + T + 2 * COLS + 8, CI), f32),
                pltpu.VMEM((Z, COLS, CI), bf16),
                pltpu.VMEM((Z, COLS, CI), bf16),
                pltpu.VMEM((Z, COLS, CI), bf16),
                pltpu.VMEM((Z, COLS, CI), bf16),
                pltpu.VMEM((T, out), f32),
                dma((6,)), dma((2, X)), dma((2, X)), dma((2, X)), dma((2, X)),
                dma((Z, NI)), dma((Z, NI)), dma((Z, NI)),
                dma((G, Z, NI)), dma((G, Z, NI)), dma((G, Z, NI)), dma((G, Z, NI)),
                dma((2,)), dma((2,)),
            ],
            compiler_params=pltpu.CompilerParams(
                collective_id=0, has_side_effects=True, vmem_limit_bytes=60 * 1024 * 1024
            ),
        )(queries[0], key_states[0], value_states[0], residual[0], proj_weight, flat)
        return result[None]

    return jax.shard_map(
        body,
        mesh=mesh,
        in_specs=(
            P(("groups", "batch"), "blk", None),
            P(("groups", "batch"), "blk", None),
            P(("groups", "batch"), "blk", None),
            P(("groups", "batch"), "blk", None),
            P(None, "batch"),
            P(None, None, "batch", None),
        ),
        out_specs=P(("groups", "batch"), "blk", None),
        check_vma=False,
    )
```

time: 160 us -> 57.3 us (0.36)
  waiting for transfers between devices: 101 us -> 0 us
  Pallas kernels: 0 us -> 53.6 us
  starting transfers between devices: 14.1 us -> 0 us
  between operations: 13.7 us -> 0.01 us
  matrix products: 9.04 us -> 0 us
  blocking collectives: 8.9 us -> 0 us
  local copies, waits for them, and re-layouts: 11.2 us -> 3.55 us
    all_gather x2 -> x0, waiting for transfers between devices: 80.7 us -> none  [the longest x1 80.7 us: body(): shard_piece = lax.all_gather(conv_weight, 'batch', axis=2, tiled=True)]
    pallas_call x0 -> x1, Pallas kernels: none -> 53.6 us  [body(): pl.pallas_call(functools.partial(kernel, G, Z, B, CI, NC), out_shape=jax....]
    all_to_all x3 -> x0, waiting for transfers between devices: 17.1 us -> none  [the longest x1 5.92 us: body(): lax.all_to_all(value_rows, 'blk', split_axis=1, concat_axis=0, tiled=True)]
    all_to_all x3 -> x0, starting transfers between devices: 11.1 us -> none  [the longest x1 4.24 us: body(): lax.all_to_all(query_rows, 'blk', split_axis=1, concat_axis=0, tiled=True)]
    dot_general x4 -> x0, matrix products: 9.04 us -> none  [the longest x1 4.48 us: body(): conv_sum = jnp.dot(stacked, flat_weight, preferred_element_type=jnp.float32)]
    all_to_all x1 -> x0, blocking collectives: 8.9 us -> none  [body(): lax.all_to_all(mixed_rows, 'blk', split_axis=0, concat_axis=1, tiled=True)]
    all_to_all x7 -> x0, local copies, waits for them, and re-layouts: 3.79 us -> none  [the longest x2 1.89 us: body(): lax.all_to_all(query_rows, 'blk', split_axis=1, concat_axis=0, tiled=True)]
    ppermute x2 -> x0, starting transfers between devices: 2.96 us -> none  [the longest x1 1.67 us: extended(): lax.ppermute(tail, axis, [(i, (i + 1) % count) for i in range(ends)])]
  transfers between devices with their start and end apart: 7 -> 0, of which waited for: 5 -> 0; matrix products, arithmetic and copies ran while one was open for 10% -> 0% of each run, Pallas kernels for 0% -> 0%
where the time goes in v1:
time: 57.3 us; the launch traced here: 57.1 us
  Pallas kernels  53.6 us (94%)
  local copies, waits for them, and re-layouts  3.55 us (6%)
    pallas_call x1, Pallas kernels, body(): pl.pallas_call(functools.partial(kernel, G, Z, B, CI, NC), out_shape=jax....  53.6 us
    unnamed x2, local copies, waits for them, and re-layouts  3.55 us

profile of v1, /device:TPU:0, one launch (start us, length us, event | category | flops | bytes accessed | tf_op | source)
XLA Modules:
  0.0 57.1 jit_solution(1159063779868746201)
XLA Ops:
  0.0 2.0 %copy.7.p_hbm = bf16[1024,192]{1,0:T(8,128)(2,1)} copy(bf16[1024,192]{0,1:T(8,128)(2,1)} %param.10) | data formatting | bytes 786432 | tf_op args[4]
  2.0 53.6 %shard_map.64 = bf16[148,384]{1,0:T(8,128)(2,1)} custom-call(bf16[148,1024]{1,0:T(8,128)(2,1)} %bitcast.8, bf16[148,1024]{1,0:T(8,128)(2,1)} %bitcast.9, bf16[148,1024]{1,0:T(8,128)(2,1)} %bitcast.10, bf16[148,768]{1,0:T(8,128)(2,1)} %bitcast.11, bf16[1024,192]{1,0:T(8,128)(2,1)} %copy.7.p_hbm, bf16[1728,384]{1,0:T(8,128)(2,1)} %bitcast.6), custom_call_target="tpu_custom_call" | custom-call | tf_op jit(solution)/shard_map/pallas_call | solution.py:345
  55.6 1.6 %copy.9 = bf16[1,148,384]{2,1,0:T(8,128)(2,1)} copy(bf16[1,148,384]{2,1,0:T(8,128)(2,1)} %bitcast.7) | data formatting | bytes 227328

commit v2 on v1

--- a/solution.py
+++ b/solution.py
@@ -26,7 +26,7 @@
     x = b // 2
     mate = x * 2 + 1 - c
     NI = 1 + NC
-    PP = wp.shape[1] // (2 * G)
+    PP = wp.shape[2] // (2 * G)
     PC = wc.shape[1] // (2 * G)
     CC = PC // NC
 
@@ -87,7 +87,7 @@
 
     def item(j, s, p):
         if j == 0:
-            return wp.at[s, pl.ds(pl.multiple_of(p * PP, 16), PP)]
+            return wp.at[s, :, pl.ds(pl.multiple_of(p * PP, 128), PP)]
         return wc.at[s, pl.ds(pl.multiple_of(p * PC + (j - 1) * CC, 16), CC)]
 
     mine = g * 2 + c
@@ -120,11 +120,9 @@
         for i in range(1, X):
             kv_out(w, i).start()
         kv_mate(w, 0).start()
-    locals_[2].wait()
-    locals_[3].wait()
-    for j in range(NI):
-        pl.when(z < Z - 1)(lambda j=j: up(j, z).start())
-        pl.when(z > 0)(lambda j=j: down(j, z).start())
+    def launch(j):
+        pl.when(z < Z - 1)(lambda: up(j, z).start())
+        pl.when(z > 0)(lambda: down(j, z).start())
 
     def arrived(j, d):
         @pl.when(z >= d)
@@ -158,13 +156,22 @@
             kv_in(w, i).wait_recv()
             kv_mate(w, i).start()
 
-    for d in range(1, Z):
+    locals_[2].wait()
+    launch(0)
+    locals_[3].wait()
+    launch(1)
+    arrived(0, 1)
+    for j in range(2, NI):
+        launch(j)
+        if j < Z:
+            arrived(0, j)
+        arrived(j - 1, 1)
+    kv_pass(0)
+    for d in range(max(NI, 2), Z):
         arrived(0, d)
-    kv_pass(0)
-    for j in range(1, NI):
-        arrived(j, 1)
+    arrived(NI - 1, 1)
     kv_pass(1)
-    for d in range(1, Z):
+    for d in range(1, min(3, Z)):
         relayed(0, d)
     for w in range(2):
         for i in range(X):
@@ -206,6 +213,8 @@
     if Z > 2:
         for j in range(2, NI):
             arrived(j, 2)
+    for d in range(3, Z):
+        relayed(0, d)
     for j in range(1, NI):
         relayed(j, 1)
 
@@ -217,7 +226,8 @@
                     cross_in(0, s, i).wait_recv()
     own = BASE + COLS
     for s in range(Z):
-        hidden = jnp.dot(att[...], wp[s], preferred_element_type=jnp.float32)
+        hidden = lax.dot_general(att[...], wp[s], (((1,), (1,)), ((), ())),
+                                 preferred_element_type=jnp.float32)
         hidden = hidden + res[:, s * CI:(s + 1) * CI].astype(jnp.float32)
         hidden = hidden.astype(jnp.bfloat16)
         wide = hidden.astype(jnp.float32)
@@ -236,14 +246,6 @@
     pl.when(b > 0)(lambda: to_prev(b - 1).start())
     pl.when(b < B - 1)(lambda: to_next(b + 1).start())
 
-    for d in range(3, Z):
-        for j in range(1, NI):
-            arrived(j, d)
-            relayed(j, d - 1)
-    if Z > 2:
-        for j in range(1, NI):
-            relayed(j, Z - 1)
-
     @pl.when(b > 0)
     def _():
         to_next(b - 1).wait_recv()
@@ -270,15 +272,13 @@
     inside = (column != 0, None, column != COLS - 1)
     acc[...] = jnp.zeros_like(acc)
 
-    def conv(n, carry):
+    def conv(n):
         s = jnp.where(z * 2 < Z, lax.rem(z + n, Z), lax.rem(z - n + Z, Z))
 
-        @pl.when(n > 0)
-        def _():
+        if n > 0:
             for j in range(1, NI):
                 for i in range(G):
                     cross_in(j, s, i).wait_recv()
-
         total = acc[...]
         for row in range(3):
             for col in range(3):
@@ -290,9 +290,19 @@
                 total = total + jnp.dot(window.astype(jnp.bfloat16), wc[s, tap * CI:(tap + 1) * CI, :],
                                         preferred_element_type=jnp.float32)
         acc[...] = total
-        return carry
-
-    lax.fori_loop(0, Z, conv, 0)
+
+    for n in range(Z):
+        conv(n)
+        if n > 0:
+            for j in range(2, NI):
+                if n + 1 < Z:
+                    relayed(j, n + 1)
+                if n + 2 < Z:
+                    arrived(j, n + 2)
+        if n + 3 < Z:
+            arrived(1, n + 3)
+        if n + 2 < Z:
+            relayed(1, n + 2)
     o_ref[...] = acc[...].astype(jnp.bfloat16)
 
     for w in range(2):
@@ -352,7 +362,7 @@
                 pltpu.VMEM((T, wide), bf16),
                 pltpu.VMEM((B, T, depth), bf16),
                 pltpu.VMEM((B, T, depth), bf16),
-                pltpu.VMEM((Z, depth, CI), bf16),
+                pltpu.VMEM((Z, CI, depth), bf16),
                 pltpu.VMEM((Z, rows, out), bf16),
                 pltpu.VMEM((T, depth), bf16),
                 pltpu.VMEM((Z, BASE + T + 2 * COLS + 8, CI), f32),
@@ -369,7 +379,7 @@
             compiler_params=pltpu.CompilerParams(
                 collective_id=0, has_side_effects=True, vmem_limit_bytes=60 * 1024 * 1024
             ),
-        )(queries[0], key_states[0], value_states[0], residual[0], proj_weight, flat)
+        )(queries[0], key_states[0], value_states[0], residual[0], proj_weight.T, flat)
         return result[None]
 
     return jax.shard_map(

time: 57.3 us -> 50.8 us (0.89)
  Pallas kernels: 53.6 us -> 49.1 us
  local copies, waits for them, and re-layouts: 3.55 us -> 1.56 us
    pallas_call x1, Pallas kernels: 53.6 us -> 49.1 us  [body(): pl.pallas_call(functools.partial(kernel, G, Z, B, CI, NC), out_shape=jax....]
    unnamed x2 -> x1, local copies, waits for them, and re-layouts: 3.55 us -> 1.56 us
where the time goes in v2:
time: 50.8 us; the launch traced here: 50.7 us
  Pallas kernels  49.1 us (97%)
  local copies, waits for them, and re-layouts  1.56 us (3%)
    pallas_call x1, Pallas kernels, body(): pl.pallas_call(functools.partial(kernel, G, Z, B, CI, NC), out_shape=jax....  49.1 us
    unnamed x1, local copies, waits for them, and re-layouts  1.56 us

profile of v2, /device:TPU:0, one launch (start us, length us, event | category | flops | bytes accessed | tf_op | source)
XLA Modules:
  0.0 50.7 jit_solution(5924524355981891531)
XLA Ops:
  0.0 49.1 %shard_map.64 = bf16[148,384]{1,0:T(8,128)(2,1)} custom-call(bf16[148,1024]{1,0:T(8,128)(2,1)} %bitcast.10, bf16[148,1024]{1,0:T(8,128)(2,1)} %bitcast.11, bf16[148,1024]{1,0:T(8,128)(2,1)} %bitcast.12, bf16[148,768]{1,0:T(8,128)(2,1)} %bitcast.13, bf16[192,1024]{1,0:T(8,128)(2,1)} %bitcast.9, bf16[1728,384]{1,0:T(8,128)(2,1)} %bitcast.7), custom_call_target="tpu_custom_call" | custom-call | tf_op jit(solution)/shard_map/pallas_call | solution.py:355
  49.1 1.6 %copy.8 = bf16[1,148,384]{2,1,0:T(8,128)(2,1)} copy(bf16[1,148,384]{2,1,0:T(8,128)(2,1)} %bitcast.8) | data formatting | bytes 227328

commit v3 on v2

--- a/solution.py
+++ b/solution.py
@@ -90,29 +90,37 @@
             return wp.at[s, :, pl.ds(pl.multiple_of(p * PP, 128), PP)]
         return wc.at[s, pl.ds(pl.multiple_of(p * PC + (j - 1) * CC, 16), CC)]
 
-    mine = g * 2 + c
+    def along_x(j):
+        return X == G and NI > 2 and j == NI - 1
+
+    def place(j):
+        return x if along_x(j) else g
+
+    def peer(j, n):
+        return {"blk": n * 2 + c} if along_x(j) else {"groups": n}
+
 
     def up(j, s):
-        return remote(item(j, s, mine), zup.at[s, j], zrecv.at[s, j], {"batch": z + 1})
+        return remote(item(j, s, place(j) * 2 + c), zup.at[s, j], zrecv.at[s, j], {"batch": z + 1})
 
     def down(j, s):
-        return remote(item(j, s, mine), zdn.at[s, j], zrecv.at[s, j], {"batch": z - 1})
+        return remote(item(j, s, place(j) * 2 + c), zdn.at[s, j], zrecv.at[s, j], {"batch": z - 1})
 
     def side(j, s, i):
-        return remote(item(j, s, mine), ysend.at[i, s, j], yrecv.at[i, s, j],
-                      {"groups": lax.rem(g + i, G)})
+        return remote(item(j, s, place(j) * 2 + c), ysend.at[i, s, j], yrecv.at[i, s, j],
+                      peer(j, lax.rem(place(j) + i, G)))
 
     def side_in(j, s, i):
-        other = lax.rem(g + G - i, G)
+        other = lax.rem(place(j) + G - i, G)
         return remote(item(j, s, other * 2 + c), ysend.at[i, s, j], yrecv.at[i, s, j],
-                      {"groups": other})
+                      peer(j, other))
 
     def cross(j, s, i):
-        other = lax.rem(g + G - i, G)
+        other = lax.rem(place(j) + G - i, G)
         return remote(item(j, s, other * 2 + c), csend.at[i, s, j], crecv.at[i, s, j], {"blk": mate})
 
     def cross_in(j, s, i):
-        other = lax.rem(g + G - i, G)
+        other = lax.rem(place(j) + G - i, G)
         return remote(item(j, s, other * 2 + 1 - c), csend.at[i, s, j], crecv.at[i, s, j], {"blk": mate})
 
     for w in range(2):

time: 50.8 us -> 49.6 us (0.976)
  Pallas kernels: 49.1 us -> 47.8 us
    pallas_call x1, Pallas kernels: 49.1 us -> 47.8 us  [body(): pl.pallas_call(functools.partial(kernel, G, Z, B, CI, NC), out_shape=jax....]
where the time goes in v3:
time: 49.6 us; the launch traced here: 49.4 us
  Pallas kernels  47.8 us (96%)
  local copies, waits for them, and re-layouts  1.56 us (3%)
    pallas_call x1, Pallas kernels, body(): pl.pallas_call(functools.partial(kernel, G, Z, B, CI, NC), out_shape=jax....  47.8 us
    unnamed x1, local copies, waits for them, and re-layouts  1.56 us

profile of v3, /device:TPU:0, one launch (start us, length us, event | category | flops | bytes accessed | tf_op | source)
XLA Modules:
  0.0 49.4 jit_solution(18032009555679921790)
XLA Ops:
  0.0 47.8 %shard_map.64 = bf16[148,384]{1,0:T(8,128)(2,1)} custom-call(bf16[148,1024]{1,0:T(8,128)(2,1)} %bitcast.10, bf16[148,1024]{1,0:T(8,128)(2,1)} %bitcast.11, bf16[148,1024]{1,0:T(8,128)(2,1)} %bitcast.12, bf16[148,768]{1,0:T(8,128)(2,1)} %bitcast.13, bf16[192,1024]{1,0:T(8,128)(2,1)} %bitcast.9, bf16[1728,384]{1,0:T(8,128)(2,1)} %bitcast.7), custom_call_target="tpu_custom_call" | custom-call | tf_op jit(solution)/shard_map/pallas_call | solution.py:363
  47.9 1.6 %copy.8 = bf16[1,148,384]{2,1,0:T(8,128)(2,1)} copy(bf16[1,148,384]{2,1,0:T(8,128)(2,1)} %bitcast.8) | data formatting | bytes 227328
